TPU v7x, 128 devices: a whole 4x4x4 slice. The times are simulated.
128 devices in a mesh: mem: 8 (over z_lo, y), sx: 4 (over z_hi, core), sy: 4 (over x).
Axes of the slice: x: 4, y: 4, z: 4 (z_hi: 2, z_lo: 2; z = z_hi * 2 + z_lo), core: 2. Of those that a mesh axis runs over, the one named last changes fastest.
Arguments:
- child: bfloat16 [32, 8, 192, 3072], P('mem', None, 'sx', 'sy'), may hold values from -13 to 13
Outputs:
- parent_mean: float32 [8, 64, 1024], P('mem', 'sx', 'sy')
- local_cov: float32 [64, 64, 1024], P('mem', 'sx', 'sy')
All inputs are finite; a program needn't handle non-finite values.
Results may differ from a plain program's by a relative error of at most 0.002.
Values sent between devices are 32-bit elements; how exact they have to be, the bound alone decides.
A program may use at most 192 MiB of HBM per device.

v0:
```python
import jax
import jax.numpy as jnp
import numpy as np
from jax import lax
from jax.sharding import Mesh
from jax.sharding import PartitionSpec as P

SX = ("sx_0", "sx_1")
MEM = ("mem_0", "mem_1")
MEM_SX_SY = ("mem_0", "mem_1", "sx_0", "sx_1", "sy")


def padded_2(array, sides, width):
    for axis, dim in sides:
        devices, length = (lax.axis_size(axis), array.shape[dim])
        up = [(i, (i + 1) % devices) for i in range(devices - 1)]
        down = [(j, i) for i, j in up]
        last = lax.slice_in_dim(array, length - width, length, axis=dim)
        initial = lax.slice_in_dim(array, 0, width, axis=dim)
        before = lax.ppermute(last, axis, up)
        after = lax.ppermute(initial, axis, down)
        array = jnp.concatenate([before, array, after], axis=dim)
    return array


def from_everyone(array, axis):
    copies = jnp.broadcast_to(array, (lax.axis_size(axis), *array.shape))
    return lax.all_to_all(copies, axis, split_axis=0, concat_axis=0, tiled=True)


def taken_together(array, axis):
    return from_everyone(array, axis).sum(axis=0)


def cut_along(array, dim, devices):
    shape = array.shape
    pieces = array.reshape(*shape[:dim], devices, shape[dim] // devices, *shape[dim + 1 :])
    return jnp.moveaxis(pieces, dim, 0)


def sum_at_owner(array, axis, dim):
    devices = lax.axis_size(axis)
    pieces = lax.all_to_all(cut_along(array, dim, devices), axis, 0, 0, tiled=True)
    return jnp.sum(pieces, axis=0)


def one_axis_at_a_time(array, axes):
    for axis in axes:
        array = lax.psum(array, axis)
    return array


def gaspari_table(reach):
    offsets = np.arange(-reach, reach + 1) * 1.0
    dist = np.sqrt(offsets[:, None] ** 2 + offsets[None, :] ** 2) / 2.5
    near = -0.25 * dist**5 + 0.5 * dist**4 + 0.625 * dist**3 - 5.0 / 3.0 * dist**2 + 1.0
    safe = np.maximum(dist, 0.001)
    far = (
        dist**5 / 12.0
        - 0.5 * dist**4
        + 0.625 * dist**3
        + 5.0 / 3.0 * dist**2
        - 5.0 * dist
        + 4.0
        - 2.0 / (3.0 * safe)
    )
    table = np.where(dist <= 1.0, near, np.where(dist < 2.0, far, 0.0))
    return table / table.sum()


def localize(owned, rows_dev, cols_dev):
    reach = 4
    padded = padded_2(owned, ((SX, 1), ("sy", 2)), reach)
    table = gaspari_table(reach)
    smoothed = jnp.zeros((owned.shape[0], rows_dev, cols_dev), jnp.float32)
    for first in range(2 * reach + 1):
        for second_off in range(2 * reach + 1):
            weight = float(table[first, second_off])
            if weight != 0.0:
                smoothed = (
                    smoothed
                    + weight
                    * padded[:, first : first + rows_dev, second_off : second_off + cols_dev]
                )
    return smoothed


def local(child):
    members_dev, levels, child_rows, child_cols = child.shape
    rows_dev = child_rows // 3
    cols_dev = child_cols // 3
    groups = lax.axis_size(MEM)
    members = members_dev * groups
    pairs_dev = levels * levels // groups
    level_dev = levels // groups
    device = lax.axis_index(MEM)
    parent = (
        jnp.sum(
            child.reshape(members_dev, levels, rows_dev, 3, cols_dev, 3),
            axis=(3, 5),
            dtype=jnp.float32,
        )
        / 9.0
    )
    totals = taken_together(jnp.sum(parent, axis=0), MEM)
    first_pair = device * pairs_dev
    pair_ids = first_pair + jnp.arange(pairs_dev, dtype=jnp.int32)
    diag_mask = (pair_ids // levels == pair_ids % levels).astype(jnp.float32)
    own_left = pair_ids // levels
    own_right = pair_ids % levels
    products = jnp.einsum("alxy,akxy->lkxy", parent, parent).reshape(
        levels * levels, rows_dev, cols_dev
    )
    second = sum_at_owner(products, MEM, 0)
    parent_mean = totals / members
    outer_own = jnp.take(parent_mean, own_left, axis=0) * jnp.take(parent_mean, own_right, axis=0)
    owned = (second - members * outer_own) / (members - 1)
    variance_total = one_axis_at_a_time(jnp.sum(owned * diag_mask[:, None, None]), MEM_SX_SY)
    cells = levels * rows_dev * lax.axis_size(SX) * cols_dev * lax.axis_size("sy")
    spread = variance_total / cells
    smoothed = localize(owned, rows_dev, cols_dev)
    local_cov = smoothed / (spread + 1e-06)
    mean_rows = lax.dynamic_slice_in_dim(parent_mean, device * level_dev, level_dev, 0)
    return (mean_rows, local_cov)


def solution(mesh):
    split = Mesh(
        mesh.devices.reshape(2, 4, 2, 2, mesh.shape["sy"]), ("mem_0", "mem_1", "sx_0", "sx_1", "sy")
    )
    in_specs = (P(MEM, None, SX, "sy"),)
    out_specs = (P(MEM, SX, "sy"), P(MEM, SX, "sy"))
    return jax.shard_map(local, mesh=split, in_specs=in_specs, out_specs=out_specs, check_vma=False)
```

profile of v0, /device:TPU:0, one launch (start us, length us, event | category | flops | bytes accessed | tf_op | source)
XLA Modules:
  0.0 194.3 jit_solution(8991469457047343743)
XLA Ops:
  0.6 37.3 %copy.9 = f32[4,8,48,768]{1,0,3,2:T(4,128)} copy(bf16[4,8,48,768]{3,2,1,0:T(8,128)(2,1)} %param.3) | data formatting | bytes 7077888 | tf_op jit(solution)/shard_map/convert_element_type | solution.py:98
  37.9 42.6 %reduce_sum.45 = f32[4,8,16,256]{1,0,3,2:T(4,128)} reduce(f32[4,8,16,3,256,3]{1,0,5,4,3,2:T(4,128)} %bitcast, f32[]{:T(128)} %constant.74.clone.1), dimensions={3,5}, to_apply=%region_0.0 | reduce | flops 1048576 | bytes 5242884 | tf_op jit(solution)/shard_map/reduce_sum | solution.py:98
  80.5 10.0 %multiply_reduce_fusion = f32[8,16,256]{0,2,1:T(8,128)S(1)} fusion(f32[4,8,16,256]{1,0,3,2:T(4,128)} %reduce_sum.45), kind=kLoop, calls=%fused_computation.4 | loop fusion | flops 229376 | bytes 655360 | tf_op jit(solution)/shard_map/reduce_sum | solution.py:105
  90.6 0.6 copy.10
  91.1 1.1 broadcast_in_dim.13
  92.3 5.9 %all-to-all-start = ((f32[8,8,16,256]{3,2,1,0:T(8,128)}), f32[8,8,16,256]{3,2,1,0:T(8,128)S(1)}, u32[]{:S(2)}, u32[]{:S(2)}) async-start(f32[8,8,16,256]{3,2,1,0:T(8,128)} %broadcast_in_dim.13), calls=%async_computation | async-start | bytes 2097152 | tf_op jit(solution)/shard_map/all_to_all | solution.py:28
  98.2 14.8 %convolution_bitcast_fusion = f32[8,8,16,256]{0,1,3,2:T(8,128)} fusion(f32[4,8,16,256]{1,0,3,2:T(4,128)} %reduce_sum.45), kind=kOutput, calls=%fused_computation.2 | convolution fusion | flops 2228224 | bytes 1572864 | tf_op jit(solution)/shard_map/alxy,akxy->lkxy/dot_general | solution.py:111
  113.0 9.1 %copy.11 = f32[8,8,16,256]{3,2,1,0:T(8,128)} copy(f32[8,8,16,256]{0,1,3,2:T(8,128)} %convolution_bitcast_fusion) | data formatting | bytes 2097152 | tf_op jit(solution)/shard_map/alxy,akxy->lkxy/transpose | solution.py:111
  122.2 0.0 all-to-all-done
  122.2 5.7 %all-to-all-start.1 = ((f32[8,8,16,256]{3,2,1,0:T(8,128)}), f32[8,8,16,256]{3,2,1,0:T(8,128)S(1)}, u32[]{:S(2)}, u32[]{:S(2)}) async-start(f32[8,8,16,256]{3,2,1,0:T(8,128)} %copy.11), calls=%async_computation.1 | async-start | bytes 2097152 | tf_op jit(solution)/shard_map/all_to_all | solution.py:43
  127.9 0.1 reduce_sum.47
  128.0 0.6 gather_fusion.1
  128.6 0.6 gather_fusion
  129.2 13.8 %all-to-all-done.1 = f32[8,8,16,256]{3,2,1,0:T(8,128)S(1)} async-done(((f32[8,8,16,256]{3,2,1,0:T(8,128)}), f32[8,8,16,256]{3,2,1,0:T(8,128)S(1)}, u32[]{:S(2)}, u32[]{:S(2)}) %all-to-all-start.1) | async-done | bytes 1048608 | tf_op jit(solution)/shard_map/all_to_all | solution.py:43
  143.0 0.1 reduce_sum.48
  143.1 0.7 multiply_reduce_fusion.1
  143.8 1.3 collective-permute-start.1
  145.1 3.0 %collective-permute-start = (f32[8,4,256]{2,1,0:T(4,128)S(1)}, f32[8,4,256]{2,1,0:T(4,128)S(1)}, u32[]{:S(2)}, u32[]{:S(2)}) collective-permute-start(f32[8,4,256]{2,1,0:T(4,128)S(1)} %get-tuple-element.9), channel_id=1, source_target_pairs={{0,4},{4,8},{8,12},{1,5},{5,9},{9,13},{2,6},{6,10},{10,14},{3,7},{... | collective-permute-start | bytes 98312 | tf_op jit(solution)/shard_map/ppermute | solution.py:20
  148.2 5.6 %psum.35 = f32[]{:T(128)} all-reduce(f32[]{:T(128)} %get-tuple-element.3), channel_id=1, replica_groups=mesh['mem_0'=2,'mem_1'=4,'sx_0'=2,'sx_1'=2,'sy'=4] {'mem_0'}, use_global_device_ids=true, to_apply=%region_5.7 | all-reduce | flops 1 | bytes 8 | tf_op jit(solution)/shard_map/psum | solution.py:49
  153.7 9.2 %psum.36 = f32[]{:T(128)} all-reduce(f32[]{:T(128)} %psum.35), channel_id=1, replica_groups=mesh['mem_0'=2,'mem_1'=4,'sx_0'=2,'sx_1'=2,'sy'=4] {'mem_1'}, use_global_device_ids=true, to_apply=%region_6.8 | all-reduce | flops 1 | bytes 8 | tf_op jit(solution)/shard_map/psum | solution.py:49
  162.9 7.1 %psum.37 = f32[]{:T(128)} all-reduce(f32[]{:T(128)} %psum.36), channel_id=1, replica_groups=mesh['mem_0'=2,'mem_1'=4,'sx_0'=2,'sx_1'=2,'sy'=4] {'sx_0'}, use_global_device_ids=true, to_apply=%region_7.9 | all-reduce | flops 1 | bytes 8 | tf_op jit(solution)/shard_map/psum | solution.py:49
  170.0 3.1 %psum.38 = f32[]{:T(128)} all-reduce(f32[]{:T(128)} %psum.37), channel_id=1, replica_groups=mesh['mem_0'=2,'mem_1'=4,'sx_0'=2,'sx_1'=2,'sy'=4] {'sx_1'}, use_global_device_ids=true, to_apply=%region_8.10 | all-reduce | flops 1 | bytes 8 | tf_op jit(solution)/shard_map/psum | solution.py:49
  173.1 0.0 collective-permute-done.1
  173.1 0.0 collective-permute-done
  173.2 0.1 fusion.89
  173.2 3.4 %collective-permute-start.2 = (f32[8,24,4]{2,1,0:T(8,128)S(1)}, f32[8,24,4]{2,1,0:T(8,128)S(1)}, u32[]{:S(2)}, u32[]{:S(2)}) collective-permute-start(f32[8,24,4]{2,1,0:T(8,128)S(1)} %get-tuple-element.7), channel_id=1, source_target_pairs={{0,1},{1,2},{2,3},{4,5},{5,6},{6,7},{8,9},{9,10},{10,11},{12,13},{... | collective-permute-start | bytes 9224 | tf_op jit(solution)/shard_map/ppermute | solution.py:20
  176.7 1.3 collective-permute-start.3
  178.0 0.6 constant_dynamic-slice_fusion
  178.6 12.2 %psum.39 = f32[]{:T(128)} all-reduce(f32[]{:T(128)} %psum.38), channel_id=1, replica_groups=mesh['mem_0'=2,'mem_1'=4,'sx_0'=2,'sx_1'=2,'sy'=4] {'sy'}, use_global_device_ids=true, to_apply=%region_9.11 | all-reduce | flops 1 | bytes 8 | tf_op jit(solution)/shard_map/psum | solution.py:49
  191.5 0.0 collective-permute-done.2
  191.5 0.0 collective-permute-done.3
  191.5 0.2 maximum_maximum_fusion
  191.7 2.6 %fusion.13 = f32[8,16,256]{2,1,0:T(8,128)} fusion(f32[8,16,256]{2,1,0:T(8,128)S(1)} %broadcast_multiply_fusion, f32[8,4,256]{2,1,0:T(4,128)S(1)} %collective-permute-done.1, f32[8,24,260]{2,1,0:T(8,128)S(1)} %get-tuple-element.6, f32[8,24,260]{2,1,0:T(8,128)S(1)} %get-tuple-element.5, f32[8,4,256]{2,1,0:T(4,128)S(1)} %collective-permute-done, ...), kind=kLoop, calls=%fused_computation.32 | loop fusion | flops 4784128 | bytes 8323076 | tf_op jit(solution)/shard_map/div | solution.py:122
  (9 shorter events, 0.1 us)
Async XLA Ops:
  92.3 29.9 %all-to-all-start = ((f32[8,8,16,256]{3,2,1,0:T(8,128)}), f32[8,8,16,256]{3,2,1,0:T(8,128)S(1)}, u32[]{:S(2)}, u32[]{:S(2)}) async-start(f32[8,8,16,256]{3,2,1,0:T(8,128)} %broadcast_in_dim.13), calls=%async_computation | async-start | bytes 2097152 | tf_op jit(solution)/shard_map/all_to_all | solution.py:28
  122.2 20.8 %all-to-all-start.1 = ((f32[8,8,16,256]{3,2,1,0:T(8,128)}), f32[8,8,16,256]{3,2,1,0:T(8,128)S(1)}, u32[]{:S(2)}, u32[]{:S(2)}) async-start(f32[8,8,16,256]{3,2,1,0:T(8,128)} %copy.11), calls=%async_computation.1 | async-start | bytes 2097152 | tf_op jit(solution)/shard_map/all_to_all | solution.py:43
  143.8 29.3 %collective-permute-start.1 = (f32[8,4,256]{2,1,0:T(4,128)S(1)}, f32[8,4,256]{2,1,0:T(4,128)S(1)}, u32[]{:S(2)}, u32[]{:S(2)}) collective-permute-start(f32[8,4,256]{2,1,0:T(4,128)S(1)} %get-tuple-element.10), channel_id=1, source_target_pairs={{4,0},{8,4},{12,8},{5,1},{9,5},{13,9},{6,2},{10,6},{14,10},{7,3},{... | collective-permute-start | bytes 98312 | tf_op jit(solution)/shard_map/ppermute | solution.py:21
  145.1 28.0 %collective-permute-start = (f32[8,4,256]{2,1,0:T(4,128)S(1)}, f32[8,4,256]{2,1,0:T(4,128)S(1)}, u32[]{:S(2)}, u32[]{:S(2)}) collective-permute-start(f32[8,4,256]{2,1,0:T(4,128)S(1)} %get-tuple-element.9), channel_id=1, source_target_pairs={{0,4},{4,8},{8,12},{1,5},{5,9},{9,13},{2,6},{6,10},{10,14},{3,7},{... | collective-permute-start | bytes 98312 | tf_op jit(solution)/shard_map/ppermute | solution.py:20
  173.2 18.2 %collective-permute-start.2 = (f32[8,24,4]{2,1,0:T(8,128)S(1)}, f32[8,24,4]{2,1,0:T(8,128)S(1)}, u32[]{:S(2)}, u32[]{:S(2)}) collective-permute-start(f32[8,24,4]{2,1,0:T(8,128)S(1)} %get-tuple-element.7), channel_id=1, source_target_pairs={{0,1},{1,2},{2,3},{4,5},{5,6},{6,7},{8,9},{9,10},{10,11},{12,13},{... | collective-permute-start | bytes 9224 | tf_op jit(solution)/shard_map/ppermute | solution.py:20
  176.7 14.8 %collective-permute-start.3 = (f32[8,24,4]{2,1,0:T(8,128)S(1)}, f32[8,24,4]{2,1,0:T(8,128)S(1)}, u32[]{:S(2)}, u32[]{:S(2)}) collective-permute-start(f32[8,24,4]{2,1,0:T(8,128)S(1)} %get-tuple-element.8), channel_id=1, source_target_pairs={{1,0},{2,1},{3,2},{5,4},{6,5},{7,6},{9,8},{10,9},{11,10},{13,12},{... | collective-permute-start | bytes 9224 | tf_op jit(solution)/shard_map/ppermute | solution.py:21
where the time goes:
time: 196 us; the launch traced here: 194 us
  other arithmetic  56.4 us (29%)
  local copies, waits for them, and re-layouts  50 us (26%)
  blocking collectives  37.2 us (19%)
  starting transfers between devices  20.6 us (11%)
  matrix products  14.8 us (8%)
  waiting for transfers between devices  13.8 us (7%)
    reduce_sum x1, other arithmetic, local(): jnp.sum(child.reshape(members_dev, levels, rows_dev, 3, cols_dev, 3), axi...  42.6 us
    convert_element_type x1, local copies, waits for them, and re-layouts, local(): jnp.sum(child.reshape(members_dev, levels, rows_dev, 3, cols_dev, 3), axi...  37.3 us
    psum x5, blocking collectives, one_axis_at_a_time(): array = lax.psum(array, axis)  37.2 us
    dot_general x1, matrix products, local(): jnp.einsum('alxy,akxy->lkxy', parent, parent)  14.8 us
    all_to_all x1, waiting for transfers between devices, sum_at_owner(): lax.all_to_all(cut_along(array, dim, devices), axis, 0, 0, tiled=True)  13.8 us
    reduce_sum x1, other arithmetic, local(): totals = taken_together(jnp.sum(parent, axis=0), MEM)  10 us
    transpose x1, local copies, waits for them, and re-layouts, local(): jnp.einsum('alxy,akxy->lkxy', parent, parent)  9.14 us
    ppermute x2, starting transfers between devices, padded_2(): before = lax.ppermute(last, axis, up)  6.43 us
  transfers between devices with their start and end apart: 6, of which 1 were waited for; matrix products, arithmetic and copies ran while one was open for 13% of the time, Pallas kernels for 0%

commit v1 on v0

--- a/solution.py
+++ b/solution.py
@@ -46,7 +46,7 @@
 
 def one_axis_at_a_time(array, axes):
     for axis in axes:
-        array = lax.psum(array, axis)
+        array = jnp.sum(lax.all_gather(array, axis), axis=0)
     return array
 
 

time: 196 us -> 206 us (1.051)
  local copies, waits for them, and re-layouts: 50 us -> 60.2 us
  blocking collectives: 37.2 us -> 34 us
  other arithmetic: 56.4 us -> 59.4 us
    psum x5 -> x0, blocking collectives: 37.2 us -> none  [one_axis_at_a_time(): array = lax.psum(array, axis)]
    unnamed x0 -> x5, blocking collectives: none -> 34 us
    unnamed x0 -> x25, local copies, waits for them, and re-layouts: none -> 10.2 us
    reduce_sum x0 -> x5, other arithmetic: none -> 3.02 us  [one_axis_at_a_time(): array = jnp.sum(lax.all_gather(array, axis), axis=0)]
  transfers between devices with their start and end apart: 6 -> 6, of which waited for: 1 -> 1; matrix products, arithmetic and copies ran while one was open for 13% -> 19% of each run, Pallas kernels for 0% -> 0%
where the time goes in v1:
time: 206 us; the launch traced here: 204 us
  local copies, waits for them, and re-layouts  60.2 us (29%)
  other arithmetic  59.4 us (29%)
  blocking collectives  34 us (17%)
  starting transfers between devices  20.6 us (10%)
  matrix products  14.8 us (7%)
  waiting for transfers between devices  13.8 us (7%)
    reduce_sum x1, other arithmetic, local(): jnp.sum(child.reshape(members_dev, levels, rows_dev, 3, cols_dev, 3), axi...  42.6 us
    convert_element_type x1, local copies, waits for them, and re-layouts, local(): jnp.sum(child.reshape(members_dev, levels, rows_dev, 3, cols_dev, 3), axi...  37.3 us
    unnamed x5, blocking collectives  34 us
    dot_general x1, matrix products, local(): jnp.einsum('alxy,akxy->lkxy', parent, parent)  14.8 us
    all_to_all x1, waiting for transfers between devices, sum_at_owner(): lax.all_to_all(cut_along(array, dim, devices), axis, 0, 0, tiled=True)  13.8 us
    unnamed x25, local copies, waits for them, and re-layouts  10.2 us
    reduce_sum x1, other arithmetic, local(): totals = taken_together(jnp.sum(parent, axis=0), MEM)  10 us
    transpose x1, local copies, waits for them, and re-layouts, local(): jnp.einsum('alxy,akxy->lkxy', parent, parent)  9.18 us
  transfers between devices with their start and end apart: 6, of which 1 were waited for; matrix products, arithmetic and copies ran while one was open for 19% of the time, Pallas kernels for 0%

profile of v1, /device:TPU:0, one launch (start us, length us, event | category | flops | bytes accessed | tf_op | source)
XLA Modules:
  0.0 204.4 jit_solution(1983263128387535381)
XLA Ops:
  0.6 37.3 %copy.9 = f32[4,8,48,768]{1,0,3,2:T(4,128)} copy(bf16[4,8,48,768]{3,2,1,0:T(8,128)(2,1)} %param.3) | data formatting | bytes 7077888 | tf_op jit(solution)/shard_map/convert_element_type | solution.py:98
  37.9 42.6 %reduce_sum.90 = f32[4,8,16,256]{1,0,3,2:T(4,128)} reduce(f32[4,8,16,3,256,3]{1,0,5,4,3,2:T(4,128)} %bitcast, f32[]{:T(128)} %constant.74.clone.1), dimensions={3,5}, to_apply=%region_0.0 | reduce | flops 1048576 | bytes 5242884 | tf_op jit(solution)/shard_map/reduce_sum | solution.py:98
  80.5 10.0 %multiply_reduce_fusion = f32[8,16,256]{0,2,1:T(8,128)S(1)} fusion(f32[4,8,16,256]{1,0,3,2:T(4,128)} %reduce_sum.90), kind=kLoop, calls=%fused_computation.4 | loop fusion | flops 229376 | bytes 655360 | tf_op jit(solution)/shard_map/reduce_sum | solution.py:105
  90.6 0.6 copy.10
  91.1 1.1 broadcast_in_dim.13
  92.3 5.9 %all-to-all-start = ((f32[8,8,16,256]{3,2,1,0:T(8,128)}), f32[8,8,16,256]{3,2,1,0:T(8,128)S(1)}, u32[]{:S(2)}, u32[]{:S(2)}) async-start(f32[8,8,16,256]{3,2,1,0:T(8,128)} %broadcast_in_dim.13), calls=%async_computation | async-start | bytes 2097152 | tf_op jit(solution)/shard_map/all_to_all | solution.py:28
  98.2 14.8 %convolution_bitcast_fusion = f32[8,8,16,256]{0,1,3,2:T(8,128)} fusion(f32[4,8,16,256]{1,0,3,2:T(4,128)} %reduce_sum.90), kind=kOutput, calls=%fused_computation.2 | convolution fusion | flops 2228224 | bytes 1572864 | tf_op jit(solution)/shard_map/alxy,akxy->lkxy/dot_general | solution.py:111
  113.0 0.0 copy-start.1
  113.0 0.0 copy-start
  113.0 9.2 %copy.11 = f32[8,8,16,256]{3,2,1,0:T(8,128)} copy(f32[8,8,16,256]{0,1,3,2:T(8,128)} %convolution_bitcast_fusion) | data formatting | bytes 2097152 | tf_op jit(solution)/shard_map/alxy,akxy->lkxy/transpose | solution.py:111
  122.2 0.0 all-to-all-done
  122.2 5.7 %all-to-all-start.1 = ((f32[8,8,16,256]{3,2,1,0:T(8,128)}), f32[8,8,16,256]{3,2,1,0:T(8,128)S(1)}, u32[]{:S(2)}, u32[]{:S(2)}) async-start(f32[8,8,16,256]{3,2,1,0:T(8,128)} %copy.11), calls=%async_computation.1 | async-start | bytes 2097152 | tf_op jit(solution)/shard_map/all_to_all | solution.py:43
  128.0 0.1 reduce_sum.92
  128.1 0.6 gather_fusion.1
  128.7 0.6 gather_fusion
  129.2 13.8 %all-to-all-done.1 = f32[8,8,16,256]{3,2,1,0:T(8,128)S(1)} async-done(((f32[8,8,16,256]{3,2,1,0:T(8,128)}), f32[8,8,16,256]{3,2,1,0:T(8,128)S(1)}, u32[]{:S(2)}, u32[]{:S(2)}) %all-to-all-start.1) | async-done | bytes 1048608 | tf_op jit(solution)/shard_map/all_to_all | solution.py:43
  143.1 0.1 reduce_sum.93
  143.1 0.7 multiply_reduce_fusion.1
  143.9 1.3 collective-permute-start.1
  145.2 3.0 %collective-permute-start = (f32[8,4,256]{2,1,0:T(4,128)S(1)}, f32[8,4,256]{2,1,0:T(4,128)S(1)}, u32[]{:S(2)}, u32[]{:S(2)}) collective-permute-start(f32[8,4,256]{2,1,0:T(4,128)S(1)} %get-tuple-element.9), channel_id=1, source_target_pairs={{0,4},{4,8},{8,12},{1,5},{5,9},{9,13},{2,6},{6,10},{10,14},{3,7},{... | collective-permute-start | bytes 98312 | tf_op jit(solution)/shard_map/ppermute | solution.py:20
  148.3 0.6 dynamic-slice
  148.9 0.7 dynamic-slice.1
  149.5 1.4 dynamic-update-slice
  150.9 0.6 dynamic-slice.2
  151.5 4.9 %all-reduce = f32[2]{0:T(128)S(1)} all-reduce(f32[2]{0:T(128)S(1)} %dynamic-update-slice), channel_id=1, replica_groups=mesh['mem_0'=2,'mem_1'=4,'sx_0'=2,'sx_1'=2,'sy'=4] {'mem_0'}, use_global_device_ids=true, to_apply=%add | all-reduce | flops 2 | bytes 16
  156.4 0.6 reduce_sum.95
  157.0 1.4 dynamic-update-slice.1
  158.5 0.7 dynamic-slice.3
  159.1 8.6 %all-reduce.1 = f32[4]{0:T(128)S(1)} all-reduce(f32[4]{0:T(128)S(1)} %dynamic-update-slice.1), channel_id=1, replica_groups=mesh['mem_0'=2,'mem_1'=4,'sx_0'=2,'sx_1'=2,'sy'=4] {'mem_1'}, use_global_device_ids=true, to_apply=%add.1 | all-reduce | flops 4 | bytes 32
  167.7 0.6 reduce_sum.96
  168.3 1.4 dynamic-update-slice.2
  169.7 0.6 dynamic-slice.4
  170.3 6.5 %all-reduce.2 = f32[2]{0:T(128)S(1)} all-reduce(f32[2]{0:T(128)S(1)} %dynamic-update-slice.2), channel_id=1, replica_groups=mesh['mem_0'=2,'mem_1'=4,'sx_0'=2,'sx_1'=2,'sy'=4] {'sx_0'}, use_global_device_ids=true, to_apply=%add.2 | all-reduce | flops 2 | bytes 16
  176.7 0.6 reduce_sum.97
  177.4 1.4 dynamic-update-slice.3
  178.8 2.4 %all-reduce.3 = f32[2]{0:T(128)S(1)} all-reduce(f32[2]{0:T(128)S(1)} %dynamic-update-slice.3), channel_id=1, replica_groups=mesh['mem_0'=2,'mem_1'=4,'sx_0'=2,'sx_1'=2,'sy'=4] {'sx_1'}, use_global_device_ids=true, to_apply=%add.3 | all-reduce | flops 2 | bytes 16
  181.2 0.6 reduce_sum.98
  181.8 1.4 dynamic-update-slice.4
  183.3 0.1 fusion.89
  183.4 3.4 %collective-permute-start.2 = (f32[8,24,4]{2,1,0:T(8,128)S(1)}, f32[8,24,4]{2,1,0:T(8,128)S(1)}, u32[]{:S(2)}, u32[]{:S(2)}) collective-permute-start(f32[8,24,4]{2,1,0:T(8,128)S(1)} %get-tuple-element.7), channel_id=1, source_target_pairs={{0,1},{1,2},{2,3},{4,5},{5,6},{6,7},{8,9},{9,10},{10,11},{12,13},{... | collective-permute-start | bytes 9224 | tf_op jit(solution)/shard_map/ppermute | solution.py:20
  186.8 1.3 collective-permute-start.3
  188.1 0.6 constant_dynamic-slice_fusion
  188.7 11.6 %all-reduce.4 = f32[4]{0:T(128)S(1)} all-reduce(f32[4]{0:T(128)S(1)} %dynamic-update-slice.4), channel_id=1, replica_groups=mesh['mem_0'=2,'mem_1'=4,'sx_0'=2,'sx_1'=2,'sy'=4] {'sy'}, use_global_device_ids=true, to_apply=%add.4 | all-reduce | flops 4 | bytes 32
  200.3 0.6 reduce_sum.99
  201.6 0.0 collective-permute-done.2
  201.6 0.0 collective-permute-done.3
  201.6 0.2 maximum_maximum_fusion
  201.8 2.6 %fusion.13 = f32[8,16,256]{2,1,0:T(8,128)} fusion(f32[8,16,256]{2,1,0:T(8,128)S(1)} %broadcast_multiply_fusion, f32[8,4,256]{2,1,0:T(4,128)S(1)} %collective-permute-done.1, f32[8,24,260]{2,1,0:T(8,128)S(1)} %get-tuple-element.6, f32[8,24,260]{2,1,0:T(8,128)S(1)} %get-tuple-element.5, f32[8,4,256]{2,1,0:T(4,128)S(1)} %collective-permute-done, ...), kind=kLoop, calls=%fused_computation.32 | loop fusion | flops 4784128 | bytes 8323076 | tf_op jit(solution)/shard_map/div | solution.py:122
  (24 shorter events, 0.2 us)
Async XLA Ops:
  92.3 30.0 %all-to-all-start = ((f32[8,8,16,256]{3,2,1,0:T(8,128)}), f32[8,8,16,256]{3,2,1,0:T(8,128)S(1)}, u32[]{:S(2)}, u32[]{:S(2)}) async-start(f32[8,8,16,256]{3,2,1,0:T(8,128)} %broadcast_in_dim.13), calls=%async_computation | async-start | bytes 2097152 | tf_op jit(solution)/shard_map/all_to_all | solution.py:28
  113.0 35.3 %copy-start.4 = (u32[128]{0:T(128)S(1)}, u32[128]{0:T(128)}, u32[]{:S(2)}) copy-start(u32[128]{0:T(128)} %constant.108) | copy-start | bytes 1540
  113.0 35.8 %copy-start.3 = (u32[128]{0:T(128)S(1)}, u32[128]{0:T(128)}, u32[]{:S(2)}) copy-start(u32[128]{0:T(128)} %constant.113) | copy-start | bytes 1540
  113.0 37.9 %copy-start.2 = (u32[128]{0:T(128)S(1)}, u32[128]{0:T(128)}, u32[]{:S(2)}) copy-start(u32[128]{0:T(128)} %constant.118) | copy-start | bytes 1540
  113.0 45.5 %copy-start.1 = (u32[128]{0:T(128)S(1)}, u32[128]{0:T(128)}, u32[]{:S(2)}) copy-start(u32[128]{0:T(128)} %constant.123) | copy-start | bytes 1540
  113.0 56.7 %copy-start = (u32[128]{0:T(128)S(1)}, u32[128]{0:T(128)}, u32[]{:S(2)}) copy-start(u32[128]{0:T(128)} %constant.128) | copy-start | bytes 1540
  122.2 20.8 %all-to-all-start.1 = ((f32[8,8,16,256]{3,2,1,0:T(8,128)}), f32[8,8,16,256]{3,2,1,0:T(8,128)S(1)}, u32[]{:S(2)}, u32[]{:S(2)}) async-start(f32[8,8,16,256]{3,2,1,0:T(8,128)} %copy.11), calls=%async_computation.1 | async-start | bytes 2097152 | tf_op jit(solution)/shard_map/all_to_all | solution.py:43
  143.9 39.3 %collective-permute-start.1 = (f32[8,4,256]{2,1,0:T(4,128)S(1)}, f32[8,4,256]{2,1,0:T(4,128)S(1)}, u32[]{:S(2)}, u32[]{:S(2)}) collective-permute-start(f32[8,4,256]{2,1,0:T(4,128)S(1)} %get-tuple-element.10), channel_id=1, source_target_pairs={{4,0},{8,4},{12,8},{5,1},{9,5},{13,9},{6,2},{10,6},{14,10},{7,3},{... | collective-permute-start | bytes 98312 | tf_op jit(solution)/shard_map/ppermute | solution.py:21
  145.2 38.0 %collective-permute-start = (f32[8,4,256]{2,1,0:T(4,128)S(1)}, f32[8,4,256]{2,1,0:T(4,128)S(1)}, u32[]{:S(2)}, u32[]{:S(2)}) collective-permute-start(f32[8,4,256]{2,1,0:T(4,128)S(1)} %get-tuple-element.9), channel_id=1, source_target_pairs={{0,4},{4,8},{8,12},{1,5},{5,9},{9,13},{2,6},{6,10},{10,14},{3,7},{... | collective-permute-start | bytes 98312 | tf_op jit(solution)/shard_map/ppermute | solution.py:20
  183.4 18.2 %collective-permute-start.2 = (f32[8,24,4]{2,1,0:T(8,128)S(1)}, f32[8,24,4]{2,1,0:T(8,128)S(1)}, u32[]{:S(2)}, u32[]{:S(2)}) collective-permute-start(f32[8,24,4]{2,1,0:T(8,128)S(1)} %get-tuple-element.7), channel_id=1, source_target_pairs={{0,1},{1,2},{2,3},{4,5},{5,6},{6,7},{8,9},{9,10},{10,11},{12,13},{... | collective-permute-start | bytes 9224 | tf_op jit(solution)/shard_map/ppermute | solution.py:20
  186.8 14.8 %collective-permute-start.3 = (f32[8,24,4]{2,1,0:T(8,128)S(1)}, f32[8,24,4]{2,1,0:T(8,128)S(1)}, u32[]{:S(2)}, u32[]{:S(2)}) collective-permute-start(f32[8,24,4]{2,1,0:T(8,128)S(1)} %get-tuple-element.8), channel_id=1, source_target_pairs={{1,0},{2,1},{3,2},{5,4},{6,5},{7,6},{9,8},{10,9},{11,10},{13,12},{... | collective-permute-start | bytes 9224 | tf_op jit(solution)/shard_map/ppermute | solution.py:21
